TPU v7x, 128 devices: a whole 4x4x4 slice. The times are simulated.
128 devices in a mesh: row: 8 (over z, core), col: 16 (over y, x).
Axes of the slice: x: 4, y: 4, z: 4, core: 2. Of those that a mesh axis runs over, the one named last changes fastest.
Arguments:
- clean: float32 [1344, 16384], P('row', 'col'), may hold values from -6 to 6
- noise: float32 [1344, 16384], P('row', 'col'), may hold values from -6 to 6
- bucket: int32 [64], replicated, may hold values from 0 to 31
- mod_table: float32 [1, 32, 1344], replicated, may hold values from -3 to 3
- w_first: float32 [1, 1344, 1344], P(None, 'row', 'col'), may hold values from -0.15625 to 0.15625
- w_second: float32 [1, 1344, 1344], P(None, 'col', 'row'), may hold values from -0.15625 to 0.15625
Outputs:
- grad_first: float32 [1, 1344, 1344], P(None, 'row', 'col')
- grad_second: float32 [1, 1344, 1344], P(None, 'col', 'row')
All inputs are finite; a program needn't handle non-finite values.
Results may differ from a plain program's by a relative error of at most 0.018.
Values may be sent and summed in bfloat16 or wider, within the bound.
A program may use at most 64 MiB of HBM per device.

v0:
```python
import math
import jax
import jax.numpy as jnp
from jax import lax
from jax.sharding import Mesh
from jax.sharding import PartitionSpec as P

PIX = 256
BUCKETS = 32
COL = ("col_0", "col_1")
MIX_WEIGHT = 0.3
KEEP_COEF = (1.0 - MIX_WEIGHT) / math.sqrt((1.0 - MIX_WEIGHT) ** 2 + MIX_WEIGHT**2)
ADD_COEF = MIX_WEIGHT / math.sqrt((1.0 - MIX_WEIGHT) ** 2 + MIX_WEIGHT**2)
SILU_GAIN = 1.0 / 0.596
CONTRACT_LEAD = (((0,), (0,)), ((), ()))
CONTRACT_TAIL = (((1,), (1,)), ((), ()))


def sent_to_all(value, axis):
    copies = jnp.broadcast_to(value, (lax.axis_size(axis), *value.shape))
    return lax.all_to_all(copies, axis, split_axis=0, concat_axis=0, tiled=True)


def over_copies(value, axis):
    everything = sent_to_all(value, axis)
    return jnp.sum(everything, axis=0)


def one_axis_at_a_time(value, axes):
    for axis in axes:
        value = lax.psum(value, axis)
    return value


def rows_first(arrays, axis, dims):
    turned = [jnp.moveaxis(a, dim, 0) for a, dim in zip(arrays, dims)]
    widths = [t[0].size for t in turned]
    both = jnp.concatenate([t.reshape(-1, w) for t, w in zip(turned, widths)], axis=1)
    result = lax.all_gather(both, axis, axis=0, tiled=True)
    blocks = jnp.split(result, [sum(widths[:k]) for k in range(1, len(widths))], axis=1)
    return tuple(
        (
            jnp.moveaxis(b.reshape(-1, *t.shape[1:]), 0, dim)
            for b, t, dim in zip(blocks, turned, dims)
        )
    )


def split_up(value, dim, count):
    before, after = (value.shape[:dim], value.shape[dim + 1 :])
    return jnp.moveaxis(value.reshape(*before, count, -1, *after), dim, 0)


def sum_together(arrays, axis, dims):
    count = lax.axis_size(axis)
    blocks = [split_up(a, dim, count) for a, dim in zip(arrays, dims)]
    lines = jnp.concatenate([b.reshape(count, -1) for b in blocks], axis=1)
    extent = max(16, -(-lines.shape[1] // 1024) * 8)
    lines = jnp.pad(lines, ((0, 0), (0, extent * 128 - lines.shape[1]))).reshape(-1, 128)
    ravelled, at, gathered = (lax.psum_scatter(lines, axis, tiled=True).reshape(-1), 0, [])
    for b in blocks:
        part = b[0]
        gathered.append(ravelled[at : at + part.size].reshape(part.shape))
        at += part.size
    return tuple(gathered)


def noise_levels(bucket):
    return jnp.exp(-3.0 + 5.0 * (bucket.astype(jnp.float32) + 0.5) / BUCKETS)


def silu_slope(values):
    sig = jax.nn.sigmoid(values)
    return sig * (1.0 + values * (1.0 - sig))


def bucket_gains(table, picked):
    onehot = (picked[:, None] == jnp.arange(table.shape[0], dtype=jnp.int32)[None, :]).astype(
        jnp.float32
    )
    return jnp.dot(onehot, table, preferred_element_type=jnp.float32)


def local(clean, noise, bucket, mod_table, w_first, w_second):
    rows_size = lax.axis_size("row")
    row_at = lax.axis_index("row")
    col_at = lax.axis_index(COL)
    samples = bucket.shape[0]
    own_rows = clean.shape[1]
    weight_first = w_first[0]
    weight_second = w_second[0]
    table = 1.0 + mod_table[0]
    col_first = jnp.sqrt(over_copies(jnp.sum(weight_first * weight_first, axis=0), "row") + 1.0)
    col_second = jnp.sqrt(
        one_axis_at_a_time(jnp.sum(weight_second * weight_second, axis=0), COL) + 1.0
    )
    normed_first = (weight_first / col_first[None, :]).astype(jnp.bfloat16)
    normed_second = (weight_second / col_second[None, :]).astype(jnp.bfloat16)
    chan_clean, chan_noise = (
        lax.all_to_all(
            clean.astype(jnp.bfloat16), "row", split_axis=1, concat_axis=0, tiled=True
        ).astype(clean.dtype),
        lax.all_to_all(
            noise.astype(jnp.bfloat16), "row", split_axis=1, concat_axis=0, tiled=True
        ).astype(noise.dtype),
    )
    local_clean = chan_clean.T
    local_noise = chan_noise.T
    sub_rows = own_rows // rows_size
    first_row = col_at * own_rows + row_at * sub_rows
    row_sample = (first_row + jnp.arange(sub_rows, dtype=jnp.int32)) // PIX
    row_bucket = jnp.take(bucket, row_sample)
    levels = noise_levels(row_bucket)[:, None]
    spread_root = jnp.sqrt(levels * levels + 0.25)
    state_own = ((local_clean + levels * local_noise) / spread_root).astype(jnp.bfloat16)
    target = local_clean * (2.0 * levels / spread_root) - local_noise * (0.5 / spread_root)
    gains = bucket_gains(table, row_bucket)
    part_first, part_second = rows_first((normed_first, normed_second), COL, (1, 0))
    full_first, full_second = rows_first((part_first, part_second), "row", (0, 1))
    pre_act = jnp.dot(state_own, full_first, preferred_element_type=jnp.float32)
    hidden = (jax.nn.silu(pre_act) * SILU_GAIN * gains).astype(jnp.bfloat16)
    branch = jnp.dot(hidden, full_second, preferred_element_type=jnp.float32)
    state_new = (KEEP_COEF * state_own.astype(jnp.float32) + ADD_COEF * branch).astype(jnp.bfloat16)
    grad_own = (state_new.astype(jnp.float32) - target) / samples
    dbranch = (ADD_COEF * grad_own).astype(jnp.bfloat16)
    gsecond_full = lax.dot_general(
        hidden, dbranch, CONTRACT_LEAD, preferred_element_type=jnp.float32
    )
    dhidden = lax.dot_general(
        dbranch, full_second, CONTRACT_TAIL, preferred_element_type=jnp.float32
    )
    dpre = (dhidden * gains * silu_slope(pre_act) * SILU_GAIN).astype(jnp.bfloat16)
    gfirst_full = lax.dot_general(
        state_own, dpre, CONTRACT_LEAD, preferred_element_type=jnp.float32
    )
    part_gfirst, part_gsecond = (
        lax.psum_scatter(
            gfirst_full.astype(jnp.bfloat16), COL, scatter_dimension=1, tiled=True
        ).astype(jnp.float32),
        lax.psum_scatter(
            gsecond_full.astype(jnp.bfloat16), COL, scatter_dimension=0, tiled=True
        ).astype(jnp.float32),
    )
    gfirst, gsecond = tuple(
        (
            part.astype(jnp.float32)
            for part in sum_together(
                (part_gfirst.astype(jnp.bfloat16), part_gsecond.astype(jnp.bfloat16)), "row", (0, 1)
            )
        )
    )
    dot_first = over_copies(jnp.sum(weight_first * gfirst, axis=0), "row")
    dot_second = one_axis_at_a_time(jnp.sum(weight_second * gsecond, axis=0), COL)
    grad_first = gfirst / col_first[None, :] - weight_first * (dot_first / col_first**3)[None, :]
    grad_second = (
        gsecond / col_second[None, :] - weight_second * (dot_second / col_second**3)[None, :]
    )
    return (grad_first[None], grad_second[None])


def solution(mesh):
    torus = Mesh(mesh.devices.reshape(mesh.shape["row"], 4, 4), ("row", "col_0", "col_1"))
    in_specs = (P("row", COL), P("row", COL), P(), P(), P(None, "row", COL), P(None, COL, "row"))
    out_specs = (P(None, "row", COL), P(None, COL, "row"))
    return jax.shard_map(local, mesh=torus, in_specs=in_specs, out_specs=out_specs, check_vma=False)
```

profile of v0, /device:TPU:1, one launch (start us, length us, event | category | flops | bytes accessed | tf_op | source)
XLA Modules:
  0.0 332.8 jit_solution(9308178163140917538)
XLA Ops:
  7.2 0.9 fusion.63
  8.1 0.6 broadcast_in_dim.11
  8.7 6.8 %all-to-all-start.2 = ((f32[8,1,84]{2,1,0:T(1,128)}), f32[8,1,84]{2,1,0:T(1,128)S(1)}, u32[]{:S(2)}, u32[]{:S(2)}) async-start(f32[8,1,84]{2,1,0:T(1,128)} %broadcast_in_dim.11), calls=%async_computation.2 | async-start | bytes 8192 | tf_op jit(solution)/shard_map/all_to_all | solution.py:21
  15.5 1.0 copy.37
  16.5 0.1 fusion.60
  16.6 8.7 %psum.28 = f32[168]{0:T(256)S(1)} all-reduce(f32[168]{0:T(256)S(1)} %fusion.60), channel_id=1, replica_groups=mesh['row'=8,'col_0'=4,'col_1'=4] {'col_0'}, use_global_device_ids=true, to_apply=%region_3.0 | all-reduce | flops 168 | bytes 1344 | tf_op jit(solution)/shard_map/psum | solution.py:31
  25.3 8.5 %psum.29 = f32[168]{0:T(256)S(1)} all-reduce(f32[168]{0:T(256)S(1)} %psum.28), channel_id=1, replica_groups=mesh['row'=8,'col_0'=4,'col_1'=4] {'col_1'}, use_global_device_ids=true, to_apply=%region_4.0 | all-reduce | flops 168 | bytes 1344 | tf_op jit(solution)/shard_map/psum | solution.py:31
  33.8 0.1 fusion.61
  34.0 0.9 fusion.66
  34.9 0.1 copy.38
  35.0 17.3 %all-gather = bf16[16,84,336]{2,1,0:T(8,128)(2,1)S(1)} all-gather(bf16[1,84,336]{2,1,0:T(8,128)(2,1)S(1)} %copy.38), channel_id=1, replica_groups=mesh['row'=8,'col_0'=4,'col_1'=4] {'col_0','col_1'}, dimensions={0}, use_global_device_ids=true | all-gather | bytes 959616 | tf_op jit(solution)/shard_map/all_gather | solution.py:39
  52.3 0.4 reshape.265
  52.7 0.3 slice_bitcast_fusion.1
  53.0 0.2 pad_maximum_fusion
  53.3 1.8 copy.39
  55.1 0.8 copy_bitcast_fusion.2
  55.9 13.5 %all-to-all-start = ((bf16[168,8,128]{2,0,1:T(8,128)(2,1)}), bf16[168,8,128]{2,0,1:T(8,128)(2,1)S(1)}, u32[]{:S(2)}, u32[]{:S(2)}) async-start(bf16[168,8,128]{2,0,1:T(8,128)(2,1)} %copy_bitcast_fusion.2), calls=%async_computation | async-start | bytes 688128 | tf_op jit(solution)/shard_map/all_to_all | solution.py:100
  69.4 1.2 gather_fusion
  70.7 0.8 copy_bitcast_fusion.1
  71.5 5.1 %all-to-all-done = bf16[168,8,128]{2,0,1:T(8,128)(2,1)S(1)} async-done(((bf16[168,8,128]{2,0,1:T(8,128)(2,1)}), bf16[168,8,128]{2,0,1:T(8,128)(2,1)S(1)}, u32[]{:S(2)}, u32[]{:S(2)}) %all-to-all-start) | async-done | bytes 344096 | tf_op jit(solution)/shard_map/all_to_all | solution.py:100
  76.6 4.5 %all-to-all-start.1 = ((bf16[168,8,128]{2,0,1:T(8,128)(2,1)}), bf16[168,8,128]{2,0,1:T(8,128)(2,1)S(1)}, u32[]{:S(2)}, u32[]{:S(2)}) async-start(bf16[168,8,128]{2,0,1:T(8,128)(2,1)} %copy_bitcast_fusion.1), calls=%async_computation.1 | async-start | bytes 688128 | tf_op jit(solution)/shard_map/all_to_all | solution.py:103
  81.2 11.6 %all-to-all-done.1 = bf16[168,8,128]{2,0,1:T(8,128)(2,1)S(1)} async-done(((bf16[168,8,128]{2,0,1:T(8,128)(2,1)}), bf16[168,8,128]{2,0,1:T(8,128)(2,1)S(1)}, u32[]{:S(2)}, u32[]{:S(2)}) %all-to-all-start.1) | async-done | bytes 344096 | tf_op jit(solution)/shard_map/all_to_all | solution.py:103
  92.8 0.2 fusion.48
  93.0 19.6 %all-gather.3.cloned.1.call-done = bf16[1344,2688]{1,0:T(8,128)(2,1)} async-done(((bf16[168,2688]{1,0:T(8,128)(2,1)}), bf16[1344,2688]{1,0:T(8,128)(2,1)}) %all-gather.3.cloned.1.call-update) | async-done | bytes 7225360 | tf_op jit(solution)/shard_map/all_gather | solution.py:39
  112.7 3.9 %fusion.2 = f32[128,1344]{0,1:T(8,128)S(1)} fusion(bf16[1344,128]{1,0:T(8,128)(2,1)S(1)} %get-tuple-element.12, bf16[1344,2688]{1,0:T(8,128)(2,1)} %all-gather.3.cloned.1.call-done), kind=kOutput, calls=%fused_computation.3 | convolution fusion | flops 462422016 | bytes 4816896 | tf_op jit(solution)/shard_map/dot_general | solution.py:120
  116.5 1.2 multiply_convert_fusion
  117.8 1.6 fusion.38
  119.4 3.1 convolution_convert_fusion
  122.5 8.7 %convolution_convert_fusion.1 = bf16[1344,1344]{0,1:T(8,128)(2,1)} fusion(bf16[1344,128]{1,0:T(8,128)(2,1)S(1)} %get-tuple-element.12, f32[128,1344]{0,1:T(8,128)S(1)} %copy-done.8, bf16[128,1344]{0,1:T(8,128)(2,1)S(1)} %fusion.38, bf16[1344,2688]{1,0:T(8,128)(2,1)} %all-gather.3.cloned.1.call-done, f32[128,1344]{0,1:T(8,128)S(1)} %fusion.2), kind=kOutput, calls=%fused_computation.2 | convolution fusion | flops 928542720 | bytes 9461760 | tf_op jit(solution)/shard_map/dot_general | solution.py:133
  131.2 101.1 %fusion.75 = (bf16[96,1344]{1,0:T(8,128)(2,1)S(1)}, bf16[1344,96]{0,1:T(8,128)(2,1)S(1)}) fusion(bf16[1344,1344]{1,0:T(8,128)(2,1)} %convolution_convert_fusion, bf16[1344,1344]{0,1:T(8,128)(2,1)} %convolution_convert_fusion.1), kind=kCustom, calls=%all-reduce-scatter.2 | all-reduce-scatter fusion | flops 4128769 | bytes 7741952
  232.3 2.8 collective-permute-start
  235.2 1.3 collective-permute-start.1
  236.5 4.2 %collective-permute-start.2 = (bf16[96,1344]{1,0:T(8,128)(2,1)S(1)}, bf16[96,1344]{1,0:T(8,128)(2,1)S(1)}, u32[]{:S(2)}, u32[]{:S(2)}) collective-permute-start(bf16[96,1344]{1,0:T(8,128)(2,1)S(1)} %get-tuple-element.4), channel_id=1, source_target_pairs={{0,1},{1,2},{2,3},{3,4},{4,5},{5,6},{6,7},{7,8},{8,9},{9,10},{10,1... | collective-permute-start | bytes 774152
  240.8 0.6 dynamic-slice.6
  242.0 0.1 slice.13
  242.1 2.7 collective-permute-start.3
  244.8 0.3 collective-permute-done.1
  245.2 3.1 concatenate.12
  248.3 0.1 constant_dynamic-slice_fusion.1
  248.4 0.2 copy.40
  248.6 0.2 reshape_reshape.3
  248.9 7.4 %collective-permute-done.3 = bf16[84,1344]{1,0:T(8,128)(2,1)S(1)} collective-permute-done((bf16[84,1344]{1,0:T(8,128)(2,1)S(1)}, bf16[84,1344]{1,0:T(8,128)(2,1)S(1)}, u32[]{:S(2)}, u32[]{:S(2)}) %collective-permute-start.3) | collective-permute-done | bytes 225824
  256.3 3.1 concatenate.13
  259.4 0.1 constant_dynamic-slice_fusion
  259.5 0.5 reshape.246
  260.0 0.1 copy.49
  260.1 0.3 reshape.247
  260.4 0.1 fusion.53
  260.5 1.0 reshape.248
  261.6 29.3 %reduce-scatter.6.cloned.1.call-done = bf16[224,128]{1,0:T(8,128)(2,1)} async-done(((bf16[1792,128]{1,0:T(8,128)(2,1)}), bf16[224,128]{1,0:T(8,128)(2,1)}) %reduce-scatter.6.cloned.1.call-update) | async-done | bytes 57360 | tf_op jit(solution)/shard_map/reduce_scatter | solution.py:60
  290.8 0.9 slice_convert_fusion
  291.7 0.1 reshape.255
  291.9 0.2 reshape.254
  292.1 0.1 copy.43
  292.2 0.1 fusion.62
  292.3 8.6 %psum.30 = f32[168]{0:T(256)S(1)} all-reduce(f32[168]{0:T(256)S(1)} %fusion.62), channel_id=1, replica_groups=mesh['row'=8,'col_0'=4,'col_1'=4] {'col_0'}, use_global_device_ids=true, to_apply=%region_11.12 | all-reduce | flops 168 | bytes 1344 | tf_op jit(solution)/shard_map/psum | solution.py:31
  300.9 8.4 %psum.31 = f32[168]{0:T(256)S(1)} all-reduce(f32[168]{0:T(256)S(1)} %psum.30), channel_id=1, replica_groups=mesh['row'=8,'col_0'=4,'col_1'=4] {'col_1'}, use_global_device_ids=true, to_apply=%region_12.13 | all-reduce | flops 168 | bytes 1344 | tf_op jit(solution)/shard_map/psum | solution.py:31
  309.3 0.2 reshape.253
  309.5 0.6 broadcast_in_dim.12
  310.1 10.6 %all-to-all-start.3 = ((f32[8,1,84]{2,1,0:T(1,128)}), f32[8,1,84]{2,1,0:T(1,128)S(1)}, u32[]{:S(2)}, u32[]{:S(2)}) async-start(f32[8,1,84]{2,1,0:T(1,128)} %broadcast_in_dim.12), calls=%async_computation.4 | async-start | bytes 8192 | tf_op jit(solution)/shard_map/all_to_all | solution.py:21
  320.7 0.7 divide_subtract_fusion
  321.4 0.2 reshape.252
  321.6 3.6 %all-to-all-done.3 = f32[8,1,84]{2,1,0:T(1,128)S(1)} async-done(((f32[8,1,84]{2,1,0:T(1,128)}), f32[8,1,84]{2,1,0:T(1,128)S(1)}, u32[]{:S(2)}, u32[]{:S(2)}) %all-to-all-start.3) | async-done | bytes 2720 | tf_op jit(solution)/shard_map/all_to_all | solution.py:21
  325.3 0.7 multiply_subtract_fusion
  (38 shorter events, 0.4 us)
Async XLA Ops:
  7.2 62.3 %copy-start = (s32[64]{0:T(128)S(1)}, s32[64]{0:T(128)}, u32[]{:S(2)}) copy-start(s32[64]{0:T(128)} %param.8) | copy-start | bytes 772
  8.7 25.2 %all-to-all-start.2 = ((f32[8,1,84]{2,1,0:T(1,128)}), f32[8,1,84]{2,1,0:T(1,128)S(1)}, u32[]{:S(2)}, u32[]{:S(2)}) async-start(f32[8,1,84]{2,1,0:T(1,128)} %broadcast_in_dim.11), calls=%async_computation.2 | async-start | bytes 8192 | tf_op jit(solution)/shard_map/all_to_all | solution.py:21
  15.5 97.1 %all-gather.3.cloned.1.call-start = ((), (), s32[]{:S(2)}) async-start(), calls=%async_computation.5 | async-start | bytes 8128512 | tf_op jit(solution)/shard_map/all_gather | solution.py:39
  52.7 2.4 copy-start.2
  53.0 17.7 %copy-start.3 = (f32[168,1024]{1,0:T(8,128)S(1)}, f32[168,1024]{1,0:T(8,128)}, u32[]{:S(2)}) copy-start(f32[168,1024]{1,0:T(8,128)} %param.7) | copy-start | bytes 2064388
  55.9 20.7 %all-to-all-start = ((bf16[168,8,128]{2,0,1:T(8,128)(2,1)}), bf16[168,8,128]{2,0,1:T(8,128)(2,1)S(1)}, u32[]{:S(2)}, u32[]{:S(2)}) async-start(bf16[168,8,128]{2,0,1:T(8,128)(2,1)} %copy_bitcast_fusion.2), calls=%async_computation | async-start | bytes 688128 | tf_op jit(solution)/shard_map/all_to_all | solution.py:100
  76.6 16.2 %all-to-all-start.1 = ((bf16[168,8,128]{2,0,1:T(8,128)(2,1)}), bf16[168,8,128]{2,0,1:T(8,128)(2,1)S(1)}, u32[]{:S(2)}, u32[]{:S(2)}) async-start(bf16[168,8,128]{2,0,1:T(8,128)(2,1)} %copy_bitcast_fusion.1), calls=%async_computation.1 | async-start | bytes 688128 | tf_op jit(solution)/shard_map/all_to_all | solution.py:103
  81.1 35.4 %copy-start.7 = (f32[1,32,1344]{2,1,0:T(8,128)S(1)}, f32[1,32,1344]{2,1,0:T(8,128)}, u32[]{:S(2)}) copy-start(f32[1,32,1344]{2,1,0:T(8,128)} %param.9) | copy-start | bytes 516100
  81.1 209.7 %reduce-scatter.6.cloned.1.call-start = ((), (), s32[]{:S(2)}) async-start(), calls=%async_computation.6 | async-start | bytes 516096 | tf_op jit(solution)/shard_map/reduce_scatter | solution.py:60
  112.7 5.1 %copy-start.6 = (bf16[1344,2688]{1,0:T(8,128)(2,1)S(1)}, bf16[1344,2688]{1,0:T(8,128)(2,1)}, u32[]{:S(2)}) copy-start(bf16[1344,2688]{1,0:T(8,128)(2,1)} %all-gather.3.cloned.1.call-done) | copy-start | bytes 21676036
  119.4 3.1 copy-start.8
  131.2 109.6 %copy-start.5 = (u32[128]{0:T(128)S(1)}, u32[128]{0:T(128)}, u32[]{:S(2)}) copy-start(u32[128]{0:T(128)} %constant.95) | copy-start | bytes 1540
  232.3 12.9 %collective-permute-start = (bf16[1344,96]{0,1:T(8,128)(2,1)S(1)}, bf16[1344,96]{0,1:T(8,128)(2,1)S(1)}, u32[]{:S(2)}, u32[]{:S(2)}) collective-permute-start(bf16[1344,96]{0,1:T(8,128)(2,1)S(1)} %get-tuple-element.5), channel_id=1, source_target_pairs={{0,1},{1,2},{2,3},{3,4},{4,5},{5,6},{6,7},{7,8},{8,9},{9,10},{10,1... | collective-permute-start | bytes 774152
  235.2 10.0 %collective-permute-start.1 = (bf16[1344,84]{0,1:T(8,128)(2,1)S(1)}, bf16[1344,84]{0,1:T(8,128)(2,1)S(1)}, u32[]{:S(2)}, u32[]{:S(2)}) collective-permute-start(bf16[1344,84]{0,1:T(8,128)(2,1)S(1)} %slice.12), channel_id=1, source_target_pairs={{0,2},{1,3},{2,4},{3,5},{4,6},{5,7},{6,8},{7,9},{8,10},{9,11},{10,... | collective-permute-start | bytes 677384
  236.5 19.8 %collective-permute-start.2 = (bf16[96,1344]{1,0:T(8,128)(2,1)S(1)}, bf16[96,1344]{1,0:T(8,128)(2,1)S(1)}, u32[]{:S(2)}, u32[]{:S(2)}) collective-permute-start(bf16[96,1344]{1,0:T(8,128)(2,1)S(1)} %get-tuple-element.4), channel_id=1, source_target_pairs={{0,1},{1,2},{2,3},{3,4},{4,5},{5,6},{6,7},{7,8},{8,9},{9,10},{10,1... | collective-permute-start | bytes 774152
  242.1 14.2 %collective-permute-start.3 = (bf16[84,1344]{1,0:T(8,128)(2,1)S(1)}, bf16[84,1344]{1,0:T(8,128)(2,1)S(1)}, u32[]{:S(2)}, u32[]{:S(2)}) collective-permute-start(bf16[84,1344]{1,0:T(8,128)(2,1)S(1)} %slice.13), channel_id=1, source_target_pairs={{0,2},{1,3},{2,4},{3,5},{4,6},{5,7},{6,8},{7,9},{8,10},{9,11},{10,... | collective-permute-start | bytes 677384
  248.6 60.8 %copy-start.1 = (f32[1,168,84]{2,1,0:T(8,128)S(1)}, f32[1,168,84]{2,1,0:T(8,128)}, u32[]{:S(2)}) copy-start(f32[1,168,84]{2,1,0:T(8,128)} %param.10) | copy-start | bytes 169348
  248.9 71.8 %copy-start.4 = (f32[1,84,168]{2,0,1:T(1,128)S(1)}, f32[1,84,168]{2,0,1:T(1,128)}, u32[]{:S(2)}) copy-start(f32[1,84,168]{2,0,1:T(1,128)} %param.11) | copy-start | bytes 169348
  310.1 15.2 %all-to-all-start.3 = ((f32[8,1,84]{2,1,0:T(1,128)}), f32[8,1,84]{2,1,0:T(1,128)S(1)}, u32[]{:S(2)}, u32[]{:S(2)}) async-start(f32[8,1,84]{2,1,0:T(1,128)} %broadcast_in_dim.12), calls=%async_computation.4 | async-start | bytes 8192 | tf_op jit(solution)/shard_map/all_to_all | solution.py:21
Sparse Core Ops, SparseCore 0:
  55.2 57.3 all-gather.2
  261.7 29.0 reduce-scatter.5
where the time goes:
time: 334 us; the launch traced here: 333 us
  blocking collectives  153 us (46%)
  waiting for transfers between devices  77.1 us (23%)
  starting transfers between devices  46.5 us (14%)
  matrix products  18.5 us (6%)
  local copies, waits for them, and re-layouts  16.3 us (5%)
  between operations  15 us (4%)
  other arithmetic  6.88 us (2%)
    unnamed x1, blocking collectives  101 us
    psum x4, blocking collectives, one_axis_at_a_time(): value = lax.psum(value, axis)  34.1 us
    reduce_scatter x1, waiting for transfers between devices, sum_together(): lax.psum_scatter(lines, axis, tiled=True).reshape(-1)  29.3 us
    all_gather x1, waiting for transfers between devices, rows_first(): result = lax.all_gather(both, axis, axis=0, tiled=True)  19.6 us
    all_to_all x2, starting transfers between devices, sent_to_all(): return lax.all_to_all(copies, axis, split_axis=0, concat_axis=0, tiled=True)  17.4 us
    all_gather x1, blocking collectives, rows_first(): result = lax.all_gather(both, axis, axis=0, tiled=True)  17.3 us
    all_to_all x1, starting transfers between devices, local(): lax.all_to_all(clean.astype(jnp.bfloat16), 'row', split_axis=1, concat_ax...  13.5 us
    all_to_all x1, waiting for transfers between devices, local(): lax.all_to_all(noise.astype(jnp.bfloat16), 'row', split_axis=1, concat_ax...  11.6 us
  transfers between devices with their start and end apart: 10, of which 7 were waited for; matrix products, arithmetic and copies ran while one was open for 3% of the time, Pallas kernels for 0%

commit v1 on v0

--- a/solution.py
+++ b/solution.py
@@ -14,6 +14,13 @@
 SILU_GAIN = 1.0 / 0.596
 CONTRACT_LEAD = (((0,), (0,)), ((), ()))
 CONTRACT_TAIL = (((1,), (1,)), ((), ()))
+
+
+def exchange_gather(block, axis, dim):
+    size = lax.axis_size(axis)
+    shards = jnp.stack([block for _ in range(size)])
+    shards = lax.all_to_all(shards, axis, split_axis=0, concat_axis=0)
+    return jnp.concatenate(shards, axis=dim)
 
 
 def sent_to_all(value, axis):
@@ -36,7 +43,7 @@
     turned = [jnp.moveaxis(a, dim, 0) for a, dim in zip(arrays, dims)]
     widths = [t[0].size for t in turned]
     both = jnp.concatenate([t.reshape(-1, w) for t, w in zip(turned, widths)], axis=1)
-    result = lax.all_gather(both, axis, axis=0, tiled=True)
+    result = exchange_gather(both, axis, 0)
     blocks = jnp.split(result, [sum(widths[:k]) for k in range(1, len(widths))], axis=1)
     return tuple(
         (

time: 334 us -> 394 us (1.18)
  waiting for transfers between devices: 77.1 us -> 143 us
  blocking collectives: 153 us -> 134 us
  starting transfers between devices: 46.5 us -> 51.5 us
  local copies, waits for them, and re-layouts: 16.3 us -> 20.3 us
    all_to_all x0 -> x2, waiting for transfers between devices: none -> 90.8 us  [exchange_gather(): shards = lax.all_to_all(shards, axis, split_axis=0, concat_axis=0)]
    all_gather x1 -> x0, waiting for transfers between devices: 19.6 us -> none  [rows_first(): result = lax.all_gather(both, axis, axis=0, tiled=True)]
    all_gather x1 -> x0, blocking collectives: 17.3 us -> none  [rows_first(): result = lax.all_gather(both, axis, axis=0, tiled=True)]
    all_to_all x0 -> x2, starting transfers between devices: none -> 9.56 us  [exchange_gather(): shards = lax.all_to_all(shards, axis, split_axis=0, concat_axis=0)]
    all_to_all x1, waiting for transfers between devices: 11.6 us -> 5.94 us  [local(): lax.all_to_all(noise.astype(jnp.bfloat16), 'row', split_axis=1, concat_ax...]
    another operation x0 -> x2, local copies, waits for them, and re-layouts: none -> 4.57 us  [exchange_gather(): shards = jnp.stack([block for _ in range(size)])]
    unnamed x28 -> x24, local copies, waits for them, and re-layouts: 8.61 us -> 8.13 us
  transfers between devices with their start and end apart: 10 -> 11, of which waited for: 7 -> 7; matrix products, arithmetic and copies ran while one was open for 3% -> 3% of each run, Pallas kernels for 0% -> 0%
where the time goes in v1:
time: 394 us; the launch traced here: 393 us
  waiting for transfers between devices  143 us (36%)
  blocking collectives  134 us (34%)
  starting transfers between devices  51.5 us (13%)
  matrix products  20.4 us (5%)
  local copies, waits for them, and re-layouts  20.3 us (5%)
  between operations  15.1 us (4%)
  other arithmetic  7.99 us (2%)
    unnamed x1, blocking collectives  100 us
    all_to_all x2, waiting for transfers between devices, exchange_gather(): shards = lax.all_to_all(shards, axis, split_axis=0, concat_axis=0)  90.8 us
    psum x4, blocking collectives, one_axis_at_a_time(): value = lax.psum(value, axis)  34.2 us
    reduce_scatter x1, waiting for transfers between devices, sum_together(): lax.psum_scatter(lines, axis, tiled=True).reshape(-1)  29.2 us
    all_to_all x2, starting transfers between devices, sent_to_all(): return lax.all_to_all(copies, axis, split_axis=0, concat_axis=0, tiled=True)  17.4 us
    all_to_all x1, starting transfers between devices, local(): lax.all_to_all(clean.astype(jnp.bfloat16), 'row', split_axis=1, concat_ax...  9.78 us
    unnamed x4, starting transfers between devices  9.67 us
    all_to_all x2, starting transfers between devices, exchange_gather(): shards = lax.all_to_all(shards, axis, split_axis=0, concat_axis=0)  9.56 us
  transfers between devices with their start and end apart: 11, of which 7 were waited for; matrix products, arithmetic and copies ran while one was open for 3% of the time, Pallas kernels for 0%

profile of v1, /device:TPU:1, one launch (start us, length us, event | category | flops | bytes accessed | tf_op | source)
XLA Modules:
  0.0 392.9 jit_solution(18048583715191568307)
XLA Ops:
  7.2 1.0 fusion.63
  8.2 0.6 broadcast_in_dim.11
  8.8 6.8 %all-to-all-start.2 = ((f32[8,1,84]{2,1,0:T(1,128)}), f32[8,1,84]{2,1,0:T(1,128)S(1)}, u32[]{:S(2)}, u32[]{:S(2)}) async-start(f32[8,1,84]{2,1,0:T(1,128)} %broadcast_in_dim.11), calls=%async_computation.2 | async-start | bytes 8192 | tf_op jit(solution)/shard_map/all_to_all | solution.py:28
  15.6 1.0 copy.39
  16.6 0.1 fusion.60
  16.7 8.7 %psum.28 = f32[168]{0:T(256)S(1)} all-reduce(f32[168]{0:T(256)S(1)} %fusion.60), channel_id=1, replica_groups=mesh['row'=8,'col_0'=4,'col_1'=4] {'col_0'}, use_global_device_ids=true, to_apply=%region_3.0 | all-reduce | flops 168 | bytes 1344 | tf_op jit(solution)/shard_map/psum | solution.py:38
  25.5 8.5 %psum.29 = f32[168]{0:T(256)S(1)} all-reduce(f32[168]{0:T(256)S(1)} %psum.28), channel_id=1, replica_groups=mesh['row'=8,'col_0'=4,'col_1'=4] {'col_1'}, use_global_device_ids=true, to_apply=%region_4.0 | all-reduce | flops 168 | bytes 1344 | tf_op jit(solution)/shard_map/psum | solution.py:38
  33.9 0.1 fusion.61
  34.1 0.9 fusion.66
  35.0 0.1 copy.40
  35.1 1.1 stack.4
  36.2 3.7 all-to-all-start.3
  40.0 0.8 copy_bitcast_fusion.2
  40.7 0.8 copy_bitcast_fusion.1
  41.5 12.1 %all-to-all-done.3 = bf16[16,84,336]{2,1,0:T(8,128)(2,1)S(1)} async-done(((bf16[16,84,336]{2,1,0:T(8,128)(2,1)}), bf16[16,84,336]{2,1,0:T(8,128)(2,1)S(1)}, u32[]{:S(2)}, u32[]{:S(2)}) %all-to-all-start.3) | async-done | bytes 903200 | tf_op jit(solution)/shard_map/all_to_all | solution.py:22
  53.6 9.8 %all-to-all-start = ((bf16[168,8,128]{2,0,1:T(8,128)(2,1)}), bf16[168,8,128]{2,0,1:T(8,128)(2,1)}, u32[]{:S(2)}, u32[]{:S(2)}) async-start(bf16[168,8,128]{2,0,1:T(8,128)(2,1)} %copy_bitcast_fusion.2), calls=%async_computation | async-start | bytes 688128 | tf_op jit(solution)/shard_map/all_to_all | solution.py:107
  63.4 0.4 reshape.256
  63.8 0.3 slice_bitcast_fusion.1
  64.1 6.6 %all-to-all-done = bf16[168,8,128]{2,0,1:T(8,128)(2,1)} async-done(((bf16[168,8,128]{2,0,1:T(8,128)(2,1)}), bf16[168,8,128]{2,0,1:T(8,128)(2,1)}, u32[]{:S(2)}, u32[]{:S(2)}) %all-to-all-start) | async-done | bytes 344096 | tf_op jit(solution)/shard_map/all_to_all | solution.py:107
  70.7 5.1 %all-to-all-start.1 = ((bf16[168,8,128]{2,0,1:T(8,128)(2,1)}), bf16[168,8,128]{2,0,1:T(8,128)(2,1)}, u32[]{:S(2)}, u32[]{:S(2)}) async-start(bf16[168,8,128]{2,0,1:T(8,128)(2,1)} %copy_bitcast_fusion.1), calls=%async_computation.1 | async-start | bytes 688128 | tf_op jit(solution)/shard_map/all_to_all | solution.py:110
  75.9 0.2 pad_maximum_fusion
  76.1 1.2 copy.41
  77.3 5.9 %all-to-all-done.1 = bf16[168,8,128]{2,0,1:T(8,128)(2,1)} async-done(((bf16[168,8,128]{2,0,1:T(8,128)(2,1)}), bf16[168,8,128]{2,0,1:T(8,128)(2,1)}, u32[]{:S(2)}, u32[]{:S(2)}) %all-to-all-start.1) | async-done | bytes 344096 | tf_op jit(solution)/shard_map/all_to_all | solution.py:110
  83.2 3.5 stack.5
  86.7 5.9 %all-to-all-start.4 = ((bf16[8,168,2688]{2,1,0:T(8,128)(2,1)}), bf16[8,168,2688]{2,1,0:T(8,128)(2,1)}, u32[]{:S(2)}, u32[]{:S(2)}) async-start(bf16[8,168,2688]{2,1,0:T(8,128)(2,1)} %stack.5), calls=%async_computation.4 | async-start | bytes 14450688 | tf_op jit(solution)/shard_map/all_to_all | solution.py:22
  92.6 1.2 gather_fusion
  93.9 1.3 fusion.48
  95.2 78.7 %all-to-all-done.4 = bf16[8,168,2688]{2,1,0:T(8,128)(2,1)} async-done(((bf16[8,168,2688]{2,1,0:T(8,128)(2,1)}), bf16[8,168,2688]{2,1,0:T(8,128)(2,1)}, u32[]{:S(2)}, u32[]{:S(2)}) %all-to-all-start.4) | async-done | bytes 7225376 | tf_op jit(solution)/shard_map/all_to_all | solution.py:22
  173.8 3.7 fusion.2
  177.6 1.2 multiply_convert_fusion
  178.8 3.7 fusion.38
  182.5 3.1 convolution_convert_fusion
  185.6 8.7 %convolution_convert_fusion.1 = bf16[1344,1344]{0,1:T(8,128)(2,1)} fusion(bf16[1344,128]{1,0:T(8,128)(2,1)S(1)} %get-tuple-element.12, f32[128,1344]{0,1:T(8,128)S(1)} %copy-done.7, bf16[128,1344]{0,1:T(8,128)(2,1)S(1)} %fusion.38, bf16[1344,2688]{1,0:T(8,128)(2,1)} %bitcast.12, f32[128,1344]{0,1:T(8,128)S(1)} %fusion.2), kind=kOutput, calls=%fused_computation.2 | convolution fusion | flops 928542720 | bytes 9461760 | tf_op jit(solution)/shard_map/dot_general | solution.py:140
  194.3 100.1 %fusion.75 = (bf16[96,1344]{1,0:T(8,128)(2,1)S(1)}, bf16[1344,96]{0,1:T(8,128)(2,1)S(1)}) fusion(bf16[1344,1344]{1,0:T(8,128)(2,1)} %convolution_convert_fusion, bf16[1344,1344]{0,1:T(8,128)(2,1)} %convolution_convert_fusion.1), kind=kCustom, calls=%all-reduce-scatter.2 | all-reduce-scatter fusion | flops 4128769 | bytes 7741952
  294.4 1.3 collective-permute-start
  295.8 1.6 collective-permute-start.1
  297.3 4.1 %collective-permute-start.2 = (bf16[96,1344]{1,0:T(8,128)(2,1)S(1)}, bf16[96,1344]{1,0:T(8,128)(2,1)S(1)}, u32[]{:S(2)}, u32[]{:S(2)}) collective-permute-start(bf16[96,1344]{1,0:T(8,128)(2,1)S(1)} %get-tuple-element.4), channel_id=1, source_target_pairs={{0,1},{1,2},{2,3},{3,4},{4,5},{5,6},{6,7},{7,8},{8,9},{9,10},{10,1... | collective-permute-start | bytes 774152
  301.4 0.6 dynamic-slice.6
  302.7 2.7 collective-permute-start.3
  305.5 3.1 concatenate.12
  308.7 0.3 copy.42
  309.0 0.3 reshape_reshape.3
  309.3 7.2 %collective-permute-done.3 = bf16[84,1344]{1,0:T(8,128)(2,1)S(1)} collective-permute-done((bf16[84,1344]{1,0:T(8,128)(2,1)S(1)}, bf16[84,1344]{1,0:T(8,128)(2,1)S(1)}, u32[]{:S(2)}, u32[]{:S(2)}) %collective-permute-start.3) | collective-permute-done | bytes 225824
  316.4 3.1 concatenate.13
  319.6 0.1 constant_dynamic-slice_fusion
  319.6 0.5 reshape.258
  320.2 0.3 reshape.259
  320.6 0.1 fusion.53
  320.7 1.0 reshape.260
  321.7 29.2 %reduce-scatter.6.cloned.1.call-done = bf16[224,128]{1,0:T(8,128)(2,1)} async-done(((bf16[1792,128]{1,0:T(8,128)(2,1)}), bf16[224,128]{1,0:T(8,128)(2,1)}) %reduce-scatter.6.cloned.1.call-update) | async-done | bytes 57360 | tf_op jit(solution)/shard_map/reduce_scatter | solution.py:67
  350.9 0.9 slice_convert_fusion
  351.8 0.1 reshape.267
  351.9 0.2 reshape.266
  352.1 0.1 copy.45
  352.2 0.1 fusion.62
  352.4 8.6 %psum.30 = f32[168]{0:T(256)S(1)} all-reduce(f32[168]{0:T(256)S(1)} %fusion.62), channel_id=1, replica_groups=mesh['row'=8,'col_0'=4,'col_1'=4] {'col_0'}, use_global_device_ids=true, to_apply=%region_11.12 | all-reduce | flops 168 | bytes 1344 | tf_op jit(solution)/shard_map/psum | solution.py:38
  360.9 8.4 %psum.31 = f32[168]{0:T(256)S(1)} all-reduce(f32[168]{0:T(256)S(1)} %psum.30), channel_id=1, replica_groups=mesh['row'=8,'col_0'=4,'col_1'=4] {'col_1'}, use_global_device_ids=true, to_apply=%region_12.13 | all-reduce | flops 168 | bytes 1344 | tf_op jit(solution)/shard_map/psum | solution.py:38
  369.4 0.2 reshape.265
  369.6 0.6 broadcast_in_dim.12
  370.2 10.6 %all-to-all-start.5 = ((f32[8,1,84]{2,1,0:T(1,128)}), f32[8,1,84]{2,1,0:T(1,128)S(1)}, u32[]{:S(2)}, u32[]{:S(2)}) async-start(f32[8,1,84]{2,1,0:T(1,128)} %broadcast_in_dim.12), calls=%async_computation.6 | async-start | bytes 8192 | tf_op jit(solution)/shard_map/all_to_all | solution.py:28
  380.8 0.7 divide_subtract_fusion
  381.5 0.2 reshape.264
  381.7 3.6 all-to-all-done.5
  385.4 0.7 multiply_subtract_fusion
  (38 shorter events, 0.5 us)
Async XLA Ops:
  7.2 85.4 %copy-start = (s32[64]{0:T(128)S(1)}, s32[64]{0:T(128)}, u32[]{:S(2)}) copy-start(s32[64]{0:T(128)} %param.8) | copy-start | bytes 772
  7.2 32.8 %copy-start.2 = (f32[168,1024]{1,0:T(8,128)S(1)}, f32[168,1024]{1,0:T(8,128)}, u32[]{:S(2)}) copy-start(f32[168,1024]{1,0:T(8,128)} %param.6) | copy-start | bytes 2064388
  7.2 33.6 %copy-start.3 = (f32[168,1024]{1,0:T(8,128)S(1)}, f32[168,1024]{1,0:T(8,128)}, u32[]{:S(2)}) copy-start(f32[168,1024]{1,0:T(8,128)} %param.7) | copy-start | bytes 2064388
  8.8 25.2 %all-to-all-start.2 = ((f32[8,1,84]{2,1,0:T(1,128)}), f32[8,1,84]{2,1,0:T(1,128)S(1)}, u32[]{:S(2)}, u32[]{:S(2)}) async-start(f32[8,1,84]{2,1,0:T(1,128)} %broadcast_in_dim.11), calls=%async_computation.2 | async-start | bytes 8192 | tf_op jit(solution)/shard_map/all_to_all | solution.py:28
  36.2 17.4 %all-to-all-start.3 = ((bf16[16,84,336]{2,1,0:T(8,128)(2,1)}), bf16[16,84,336]{2,1,0:T(8,128)(2,1)S(1)}, u32[]{:S(2)}, u32[]{:S(2)}) async-start(bf16[16,84,336]{2,1,0:T(8,128)(2,1)} %stack.4), calls=%async_computation.3 | async-start | bytes 2162688 | tf_op jit(solution)/shard_map/all_to_all | solution.py:22
  53.6 17.1 %all-to-all-start = ((bf16[168,8,128]{2,0,1:T(8,128)(2,1)}), bf16[168,8,128]{2,0,1:T(8,128)(2,1)}, u32[]{:S(2)}, u32[]{:S(2)}) async-start(bf16[168,8,128]{2,0,1:T(8,128)(2,1)} %copy_bitcast_fusion.2), calls=%async_computation | async-start | bytes 688128 | tf_op jit(solution)/shard_map/all_to_all | solution.py:107
  70.7 12.5 %all-to-all-start.1 = ((bf16[168,8,128]{2,0,1:T(8,128)(2,1)}), bf16[168,8,128]{2,0,1:T(8,128)(2,1)}, u32[]{:S(2)}, u32[]{:S(2)}) async-start(bf16[168,8,128]{2,0,1:T(8,128)(2,1)} %copy_bitcast_fusion.1), calls=%async_computation.1 | async-start | bytes 688128 | tf_op jit(solution)/shard_map/all_to_all | solution.py:110
  86.7 87.2 %all-to-all-start.4 = ((bf16[8,168,2688]{2,1,0:T(8,128)(2,1)}), bf16[8,168,2688]{2,1,0:T(8,128)(2,1)}, u32[]{:S(2)}, u32[]{:S(2)}) async-start(bf16[8,168,2688]{2,1,0:T(8,128)(2,1)} %stack.5), calls=%async_computation.4 | async-start | bytes 14450688 | tf_op jit(solution)/shard_map/all_to_all | solution.py:22
  92.6 258.3 %reduce-scatter.6.cloned.1.call-start = ((), (), s32[]{:S(2)}) async-start(), calls=%async_computation.7 | async-start | bytes 516096 | tf_op jit(solution)/shard_map/reduce_scatter | solution.py:67
  92.6 85.0 %copy-start.6 = (f32[1,32,1344]{2,1,0:T(8,128)S(1)}, f32[1,32,1344]{2,1,0:T(8,128)}, u32[]{:S(2)}) copy-start(f32[1,32,1344]{2,1,0:T(8,128)} %param.9) | copy-start | bytes 516100
  182.5 3.1 copy-start.7
  194.3 107.1 %copy-start.5 = (u32[128]{0:T(128)S(1)}, u32[128]{0:T(128)}, u32[]{:S(2)}) copy-start(u32[128]{0:T(128)} %constant.95) | copy-start | bytes 1540
  294.4 11.1 %collective-permute-start = (bf16[1344,96]{0,1:T(8,128)(2,1)S(1)}, bf16[1344,96]{0,1:T(8,128)(2,1)S(1)}, u32[]{:S(2)}, u32[]{:S(2)}) collective-permute-start(bf16[1344,96]{0,1:T(8,128)(2,1)S(1)} %get-tuple-element.5), channel_id=1, source_target_pairs={{0,1},{1,2},{2,3},{3,4},{4,5},{5,6},{6,7},{7,8},{8,9},{9,10},{10,1... | collective-permute-start | bytes 774152
  295.8 9.7 %collective-permute-start.1 = (bf16[1344,84]{0,1:T(8,128)(2,1)S(1)}, bf16[1344,84]{0,1:T(8,128)(2,1)S(1)}, u32[]{:S(2)}, u32[]{:S(2)}) collective-permute-start(bf16[1344,84]{0,1:T(8,128)(2,1)S(1)} %slice.12), channel_id=1, source_target_pairs={{0,2},{1,3},{2,4},{3,5},{4,6},{5,7},{6,8},{7,9},{8,10},{9,11},{10,... | collective-permute-start | bytes 677384
  297.3 19.1 %collective-permute-start.2 = (bf16[96,1344]{1,0:T(8,128)(2,1)S(1)}, bf16[96,1344]{1,0:T(8,128)(2,1)S(1)}, u32[]{:S(2)}, u32[]{:S(2)}) collective-permute-start(bf16[96,1344]{1,0:T(8,128)(2,1)S(1)} %get-tuple-element.4), channel_id=1, source_target_pairs={{0,1},{1,2},{2,3},{3,4},{4,5},{5,6},{6,7},{7,8},{8,9},{9,10},{10,1... | collective-permute-start | bytes 774152
  302.7 13.7 %collective-permute-start.3 = (bf16[84,1344]{1,0:T(8,128)(2,1)S(1)}, bf16[84,1344]{1,0:T(8,128)(2,1)S(1)}, u32[]{:S(2)}, u32[]{:S(2)}) collective-permute-start(bf16[84,1344]{1,0:T(8,128)(2,1)S(1)} %slice.13), channel_id=1, source_target_pairs={{0,2},{1,3},{2,4},{3,5},{4,6},{5,7},{6,8},{7,9},{8,10},{9,11},{10,... | collective-permute-start | bytes 677384
  309.0 60.6 %copy-start.1 = (f32[1,168,84]{2,1,0:T(8,128)S(1)}, f32[1,168,84]{2,1,0:T(8,128)}, u32[]{:S(2)}) copy-start(f32[1,168,84]{2,1,0:T(8,128)} %param.10) | copy-start | bytes 169348
  309.2 71.5 %copy-start.4 = (f32[1,84,168]{2,0,1:T(1,128)S(1)}, f32[1,84,168]{2,0,1:T(1,128)}, u32[]{:S(2)}) copy-start(f32[1,84,168]{2,0,1:T(1,128)} %param.11) | copy-start | bytes 169348
  370.2 15.2 %all-to-all-start.5 = ((f32[8,1,84]{2,1,0:T(1,128)}), f32[8,1,84]{2,1,0:T(1,128)S(1)}, u32[]{:S(2)}, u32[]{:S(2)}) async-start(f32[8,1,84]{2,1,0:T(1,128)} %broadcast_in_dim.12), calls=%async_computation.6 | async-start | bytes 8192 | tf_op jit(solution)/shard_map/all_to_all | solution.py:28
Sparse Core Ops, SparseCore 0:
  321.8 29.0 reduce-scatter.5
